TPU v7x, 1024 devices: a whole 8x8x8 slice. The times are simulated.
1024 devices in a mesh: dp: 32 (over z_hi, x, core), tensor: 32 (over z_lo, y).
Axes of the slice: x: 8, y: 8, z: 8 (z_hi: 2, z_lo: 4; z = z_hi * 4 + z_lo), core: 2. Of those that a mesh axis runs over, the one named last changes fastest.
Arguments:
- grad_out: bfloat16 [8192, 4096], P(('dp', 'tensor')), may hold values from -2.5 to 2.5
- gate_pre: bfloat16 [8192, 14848], P('dp', 'tensor'), may hold values from -8 to 8
- up_pre: bfloat16 [8192, 14848], P('dp', 'tensor'), may hold values from -6 to 6
- down_weight: bfloat16 [4096, 14848], P(None, 'tensor'), may hold values from -1.5 to 1.5
Outputs:
- grad_weight: float32 [4096, 14848], P('dp', 'tensor')
- grad_gate: bfloat16 [8192, 14848], P('dp', 'tensor')
- grad_up: bfloat16 [8192, 14848], P('dp', 'tensor')
All inputs are finite; a program needn't handle non-finite values.
Results may differ from a plain program's by a relative error of at most 0.015.
Values may be sent and summed in bfloat16 or wider, within the bound.
No kernel may reach another device: no remote copies, remote signals or barrier semaphores. Data moves between devices by JAX's collectives and lax.ppermute only.
A program may use at most 32 MiB of HBM per device.

v0:
```python
import jax
import jax.numpy as jnp
from jax import lax
from jax.sharding import PartitionSpec as P


def in_order(tiles, dim):
    shape = list(tiles.shape[1:])
    shape[dim] *= tiles.shape[0]
    return jnp.moveaxis(tiles, 0, dim).reshape(shape)


def copy_for_each(x, axis):
    size = lax.axis_size(axis)
    return lax.all_to_all(jnp.broadcast_to(x[None], (size, *x.shape)), axis, 0, 0, tiled=True)


def gather_directly(x, axis, dim):
    return in_order(copy_for_each(x, axis), dim)


def contract_rows(left, right):
    return lax.dot_general(
        left, right, (((0,), (0,)), ((), ())), preferred_element_type=jnp.float32
    )


def body(grad_out, gate_pre, up_pre, down_weight):
    gate = gate_pre.astype(jnp.float32)
    upper = up_pre.astype(jnp.float32)
    sig = jax.nn.sigmoid(gate)
    act = gate * sig
    hidden = (act * upper).astype(jnp.bfloat16)
    whole = gather_directly(grad_out, "tensor", 0)
    grad_hidden = jnp.dot(whole, down_weight, preferred_element_type=jnp.float32)
    grad_weight = lax.psum_scatter(
        contract_rows(whole, hidden).astype(jnp.bfloat16), "dp", scatter_dimension=0, tiled=True
    ).astype(jnp.float32)
    grad_up = (grad_hidden * act).astype(jnp.bfloat16)
    grad_gate = (grad_hidden * upper * sig * (1.0 + gate * (1.0 - sig))).astype(jnp.bfloat16)
    return (grad_weight, grad_gate, grad_up)


def solution(mesh):
    in_specs = (P(("dp", "tensor"), None), P("dp", "tensor"), P("dp", "tensor"), P(None, "tensor"))
    out_specs = (P("dp", "tensor"), P("dp", "tensor"), P("dp", "tensor"))
    return jax.shard_map(body, mesh=mesh, in_specs=in_specs, out_specs=out_specs, check_vma=False)
```

profile of v0, /device:TPU:4, one launch (start us, length us, event | category | flops | bytes accessed | tf_op | source)
XLA Modules:
  0.0 256.9 jit_solution(18380960744504666016)
XLA Ops:
  7.2 0.0 copy-start
  7.2 0.0 copy-start.1
  7.2 0.0 reduce-scatter.4.cloned.1.call-start
  7.2 1.2 broadcast_in_dim.2
  8.4 67.6 %all_to_all.5 = bf16[32,8,4096]{2,1,0:T(8,128)(2,1)S(1)} all-to-all(bf16[32,8,4096]{2,1,0:T(8,128)(2,1)S(1)} %broadcast_in_dim.2), channel_id=1, replica_groups=mesh['dp'=32,'tensor'=32] {'tensor'}, dimensions={0} | all-to-all | bytes 4194304 | tf_op jit(solution)/shard_map/all_to_all | solution.py:15
  76.0 0.0 copy-done
  76.0 0.0 copy-done.1
  76.0 3.1 %fusion = bf16[4096,464]{0,1:T(8,128)(2,1)} fusion(bf16[32,8,4096]{2,1,0:T(8,128)(2,1)S(1)} %all_to_all.5, bf16[256,464]{0,1:T(8,128)(2,1)S(1)} %copy-done, bf16[256,464]{0,1:T(8,128)(2,1)S(1)} %copy-done.1), kind=kOutput, calls=%fused_computation.1 | convolution fusion | flops 975929344 | bytes 6373376 | tf_op jit(solution)/shard_map/dot_general | solution.py:23
  79.1 6.4 %copy.7 = bf16[4096,464]{1,0:T(8,128)(2,1)} copy(bf16[4096,464]{0,1:T(8,128)(2,1)} %fusion) | data formatting | bytes 7602176
  85.5 0.0 reduce-scatter.4.cloned.1.call-update
  85.5 4.1 %multiply_convert_fusion = (bf16[256,464]{0,1:T(8,128)(2,1)}, bf16[256,464]{0,1:T(8,128)(2,1)}) fusion(bf16[256,464]{0,1:T(8,128)(2,1)S(1)} %copy-done.1, bf16[256,464]{0,1:T(8,128)(2,1)S(1)} %copy-done, bf16[4096,464]{0,1:T(8,128)(2,1)} %param.7, bf16[32,8,4096]{2,1,0:T(8,128)(2,1)S(1)} %all_to_all.5), kind=kOutput, calls=%fused_computation.18 | convolution fusion | flops 974860288 | bytes 6848512 | tf_op jit(solution)/shard_map/dot_general | solution.py:35
  89.6 158.6 %reduce-scatter.4.cloned.1.call-done = bf16[128,464]{1,0:T(8,128)(2,1)} async-done(((bf16[4096,464]{1,0:T(8,128)(2,1)}), bf16[128,464]{1,0:T(8,128)(2,1)}) %reduce-scatter.4.cloned.1.call-update) | async-done | bytes 118800
  248.3 1.0 copy.8
  249.3 0.7 convert_element_type.29
Async XLA Ops:
  7.2 68.8 %copy-start = (bf16[256,464]{0,1:T(8,128)(2,1)S(1)}, bf16[256,464]{0,1:T(8,128)(2,1)}, u32[]{:S(2)}) copy-start(bf16[256,464]{0,1:T(8,128)(2,1)} %param.6) | copy-start | bytes 712708
  7.2 68.8 %copy-start.1 = (bf16[256,464]{0,1:T(8,128)(2,1)S(1)}, bf16[256,464]{0,1:T(8,128)(2,1)}, u32[]{:S(2)}) copy-start(bf16[256,464]{0,1:T(8,128)(2,1)} %param.5) | copy-start | bytes 712708
  7.2 241.1 %reduce-scatter.4.cloned.1.call-start = ((), (), s32[]{:S(2)}) async-start(), calls=%async_computation.2 | async-start | bytes 4325376
Sparse Core Ops, SparseCore 0:
  85.7 162.5 reduce-scatter.3
where the time goes:
time: 257 us
  waiting for transfers between devices  159 us (62%)
  blocking collectives  67.6 us (26%)
  between operations  14.1 us (5%)
  local copies, waits for them, and re-layouts  8.65 us (3%)
  matrix products  7.16 us (3%)
    unnamed x2, waiting for transfers between devices  159 us
    all_to_all x1, blocking collectives, copy_for_each(): lax.all_to_all(jnp.broadcast_to(x[None], (size, *x.shape)), axis, 0, 0, t...  67.6 us
    unnamed x6, local copies, waits for them, and re-layouts  7.49 us
  transfers between devices with their start and end apart: 1, of which 1 were waited for; matrix products, arithmetic and copies ran while one was open for 2% of the time, Pallas kernels for 0%

commit v1 on v0

v1 whole, which is shorter than its diff:
```python
import jax
import jax.numpy as jnp
from jax import lax
from jax.sharding import Mesh, PartitionSpec as P

AXES = ("zh", "x", "c", "zl", "y")
STEPS = (64.0, 32.0, 16.0, 8.0, 4.0, 2.0)


def exponents(most):
    k = jnp.zeros_like(most)
    for bit in STEPS:
        fits = most * (2.0**bit) <= 32768.0
        most = jnp.where(fits, most * (2.0**bit), most)
        k = jnp.where(fits, k + bit, k)
    return k


def power(k, sign):
    scale = jnp.ones_like(k)
    for bit in STEPS:
        has = k >= bit
        scale = jnp.where(has, scale * (2.0 ** (sign * bit)), scale)
        k = jnp.where(has, k - bit, k)
    return scale


def coded(rows):
    n = rows.shape[0]
    wide = rows.astype(jnp.float32)
    most = jnp.max(jnp.abs(wide).reshape(n * 8, 4, 128), axis=(0, 2))
    k = jnp.repeat(exponents(most), 128)[None, None, :]
    return (wide * power(k, 1)).astype(jnp.float16), jnp.broadcast_to(k, (1, 8, 512)).astype(jnp.float16)


def body(grad_out, gate_pre, up_pre, down_weight):
    f_w = grad_out.shape[1]
    gate = gate_pre.T.astype(jnp.float32)
    upper = up_pre.T.astype(jnp.float32)
    sig = jax.nn.sigmoid(gate)
    act = gate * sig
    hidden = (act * upper).astype(jnp.bfloat16)
    h, t = hidden.shape

    split = grad_out.reshape(8, 2, 8, 256).transpose(2, 0, 1, 3).reshape(8, 8, 512)
    mine = lax.all_to_all(split, "x", 0, 0)
    own = grad_out.reshape(8, 8, 512).transpose(1, 0, 2)
    both = jnp.concatenate([own, mine], 0)
    near = lax.all_gather(both, "zl", axis=1)
    hiddens = lax.all_to_all(jnp.broadcast_to(hidden[None], (8, h, t)), "x", 0, 0)

    near = near.reshape(64, 8, 512)
    a, ka = coded(near[:32])
    b, kb = coded(near[32:])
    message = jnp.concatenate([a, b, ka, kb], 0)
    got = lax.all_gather(message, "y", axis=1, tiled=True).astype(jnp.float32)
    whole = (got[:32] * power(got[64], -1)).astype(jnp.bfloat16)
    feats = (got[32:64] * power(got[65], -1)).astype(jnp.bfloat16)
    whole = whole.reshape(8, t, 512)
    feats = feats.reshape(8, t, 512)

    part = lax.dot_general(hiddens, feats, (((0, 2), (0, 1)), ((), ())), preferred_element_type=jnp.float32)
    part = part.astype(jnp.bfloat16).reshape(h, 2, 2, 128).transpose(2, 1, 0, 3)
    part = lax.all_to_all(part, "c", 0, 0).astype(jnp.float32).sum(0).astype(jnp.bfloat16)
    part = lax.all_to_all(part, "zh", 0, 0).astype(jnp.float32).sum(0)

    weight = down_weight.T.reshape(h, 8, 512)
    grad_hidden = lax.dot_general(weight, whole, (((1, 2), (0, 2)), ((), ())), preferred_element_type=jnp.float32)
    grad_up = (grad_hidden * act).astype(jnp.bfloat16)
    grad_gate = (grad_hidden * upper * sig * (1.0 + gate * (1.0 - sig))).astype(jnp.bfloat16)
    return part.T, grad_gate.T, grad_up.T


def solution(mesh):
    dims = (2, 8, 2, 4, 8)
    fine = Mesh(mesh.devices.reshape(dims), AXES)
    dp, tensor = ("zh", "x", "c"), ("zl", "y")
    in_specs = (P(dp + tensor, None), P(dp, tensor), P(dp, tensor), P(None, tensor))
    out_specs = (P(dp, tensor), P(dp, tensor), P(dp, tensor))
    return jax.shard_map(body, mesh=fine, in_specs=in_specs, out_specs=out_specs, check_vma=False)
```

time: 257 us -> 126 us (0.49)
  the two profiles are of different devices: /device:TPU:4 before, /device:TPU:2 now
where the time goes in v1:
time: 126 us; the launch traced here: 125 us
  blocking collectives  61.4 us (49%)
  starting transfers between devices  32 us (25%)
  waiting for transfers between devices  11.7 us (9%)
  other arithmetic  8.02 us (6%)
  matrix products  7.41 us (6%)
  local copies, waits for them, and re-layouts  4.16 us (3%)
    all_gather x1, blocking collectives, body(): got = lax.all_gather(message, 'y', axis=1, tiled=True).astype(jnp.float32)  42 us
    all_to_all x1, starting transfers between devices, body(): mine = lax.all_to_all(split, 'x', 0, 0)  16.4 us
    all_gather x1, blocking collectives, body(): near = lax.all_gather(both, 'zl', axis=1)  15.4 us
    all_to_all x1, starting transfers between devices, body(): part = lax.all_to_all(part, 'zh', 0, 0).astype(jnp.float32).sum(0)  9.72 us
    all_to_all x1, waiting for transfers between devices, body(): part = lax.all_to_all(part, 'zh', 0, 0).astype(jnp.float32).sum(0)  5.92 us
    all_to_all x1, starting transfers between devices, body(): lax.all_to_all(jnp.broadcast_to(hidden[None], (8, h, t)), 'x', 0, 0)  5.87 us
    all_to_all x1, waiting for transfers between devices, body(): mine = lax.all_to_all(split, 'x', 0, 0)  5.74 us
    dot_general x1, matrix products, body(): lax.dot_general(weight, whole, (((1, 2), (0, 2)), ((), ())), preferred_el...  4.1 us
  transfers between devices with their start and end apart: 3, of which 2 were waited for; matrix products, arithmetic and copies ran while one was open for 8% of the time, Pallas kernels for 0%

profile of v1, /device:TPU:2, one launch (start us, length us, event | category | flops | bytes accessed | tf_op | source)
XLA Modules:
  0.0 125.4 jit_solution(367002928565145709)
XLA Ops:
  0.6 0.0 copy-start
  0.6 1.0 copy.37
  1.6 0.7 reshape.199
  2.3 16.4 %all-to-all-start.1 = ((bf16[8,8,512]{2,1,0:T(8,128)(2,1)}), bf16[8,8,512]{2,1,0:T(8,128)(2,1)S(1)}, u32[]{:S(2)}, u32[]{:S(2)}) async-start(bf16[8,8,512]{2,1,0:T(8,128)(2,1)} %reshape.199), calls=%async_computation.1 | async-start | bytes 131072 | tf_op jit(solution)/shard_map/all_to_all | solution.py:46
  18.7 1.2 fusion.12
  19.9 5.7 %all-to-all-done.1 = bf16[8,8,512]{2,1,0:T(8,128)(2,1)S(1)} async-done(((bf16[8,8,512]{2,1,0:T(8,128)(2,1)}), bf16[8,8,512]{2,1,0:T(8,128)(2,1)S(1)}, u32[]{:S(2)}, u32[]{:S(2)}) %all-to-all-start.1) | async-done | bytes 65568 | tf_op jit(solution)/shard_map/all_to_all | solution.py:46
  25.7 1.4 %broadcast_in_dim.10 = bf16[8,464,256]{2,1,0:T(8,128)(2,1)} broadcast(bf16[464,256]{1,0:T(8,128)(2,1)S(1)} %fusion.12), dimensions={1,2} | broadcast | bytes 2138112 | tf_op jit(solution)/shard_map/broadcast_in_dim | solution.py:50
  27.0 5.9 %all-to-all-start = ((bf16[8,464,256]{2,1,0:T(8,128)(2,1)}), bf16[8,464,256]{2,1,0:T(8,128)(2,1)}, u32[]{:S(2)}, u32[]{:S(2)}) async-start(bf16[8,464,256]{2,1,0:T(8,128)(2,1)} %broadcast_in_dim.10), calls=%async_computation | async-start | bytes 3801088 | tf_op jit(solution)/shard_map/all_to_all | solution.py:50
  32.9 0.0 copy-done
  32.9 15.4 %all-gather = bf16[16,32,512]{2,1,0:T(8,128)(2,1)S(1)} all-gather(bf16[16,8,512]{2,1,0:T(8,128)(2,1)S(1)} %pad_maximum_fusion.1), channel_id=2, replica_groups=mesh['zh'=2,'x'=8,'c'=2,'zl'=4,'y'=8] {'zl'}, dimensions={1}, use_global_device_ids=true | all-gather | bytes 655360 | tf_op jit(solution)/shard_map/all_gather | solution.py:49
  48.3 0.1 abs_reduce_fusion.1
  48.4 0.1 slice_convert_fusion.1
  48.5 0.1 bitcast_reduce_fusion
  48.7 0.1 multiply_select_fusion.15
  48.8 0.1 bitcast_convert_fusion.1
  48.9 0.1 multiply_select_fusion.10
  48.9 0.1 bitcast_convert_fusion
  49.0 0.1 multiply_convert_fusion
  49.1 0.1 multiply_convert_fusion.1
  49.2 0.2 pad_maximum_fusion
  49.4 42.0 %all-gather.2 = f16[66,64,512]{2,1,0:T(8,128)(2,1)S(1)} all-gather(f16[66,8,512]{2,1,0:T(8,128)(2,1)S(1)} %pad_maximum_fusion), channel_id=1, replica_groups=mesh['zh'=2,'x'=8,'c'=2,'zl'=4,'y'=8] {'y'}, dimensions={1}, use_global_device_ids=true | all-gather | bytes 4866048 | tf_op jit(solution)/shard_map/all_gather | solution.py:56
  91.3 1.2 convert_element_type.106
  92.5 0.2 fusion.28
  92.7 2.7 %fusion = (bf16[32,64,512]{2,1,0:T(8,128)(2,1)S(1)}, bf16[32,64,512]{2,1,0:T(8,128)(2,1)}) fusion(f32[66,64,512]{2,1,0:T(8,128)S(1)} %convert_element_type.106, f32[64,512]{1,0:T(8,128)S(1)} %get-tuple-element.7, f32[64,512]{1,0:T(8,128)S(1)} %get-tuple-element.8), kind=kLoop, calls=%fused_computation.1 | loop fusion | flops 4194304 | bytes 12845056 | tf_op jit(solution)/shard_map/convert_element_type | solution.py:57
  95.4 0.0 all-to-all-done
  95.4 3.3 %fusion.5 = bf16[464,512]{1,0:T(8,128)(2,1)S(1)} fusion(bf16[8,464,256]{2,1,0:T(8,128)(2,1)} %all-to-all-done, bf16[8,256,512]{2,1,0:T(8,128)(2,1)} %bitcast.118), kind=kOutput, calls=%fused_computation.8 | convolution fusion | flops 973316096 | bytes 4472832 | tf_op jit(solution)/shard_map/dot_general | solution.py:62
  98.7 0.0 copy-start.1
  98.7 0.0 copy-start.2
  98.7 0.1 reshape.201
  98.9 0.2 copy.36
  99.1 4.1 %all_to_all.20 = bf16[2,2,464,128]{3,1,2,0:T(2,128)(2,1)S(1)} all-to-all(bf16[2,2,464,128]{3,1,2,0:T(2,128)(2,1)S(1)} %bitcast.121), channel_id=1, replica_groups=mesh['zh'=2,'x'=8,'c'=2,'zl'=4,'y'=8] {'c'}, dimensions={0} | all-to-all | bytes 950272 | tf_op jit(solution)/shard_map/all_to_all | solution.py:64
  103.2 1.0 reduce_sum.21
  104.2 0.7 copy.22
  104.9 9.7 %all-to-all-start.3 = ((bf16[2,464,128]{2,1,0:T(8,128)(2,1)}), bf16[2,464,128]{2,1,0:T(8,128)(2,1)S(1)}, u32[]{:S(2)}, u32[]{:S(2)}) async-start(bf16[2,464,128]{2,1,0:T(8,128)(2,1)} %copy.22), calls=%async_computation.3 | async-start | bytes 475136 | tf_op jit(solution)/shard_map/all_to_all | solution.py:65
  114.7 0.0 copy-done.1
  114.7 0.0 copy-done.2
  114.7 4.1 %fusion.24 = (bf16[256,464]{0,1:T(8,128)(2,1)}, bf16[256,464]{0,1:T(8,128)(2,1)}) fusion(bf16[256,464]{0,1:T(8,128)(2,1)S(1)} %copy-done.2, bf16[256,464]{0,1:T(8,128)(2,1)S(1)} %copy-done.1, bf16[8,256,512]{2,1,0:T(8,128)(2,1)S(1)} %bitcast.117, bf16[58,8,8,512]{3,2,1,0:T(8,128)(2,1)} %bitcast.126), kind=kOutput, calls=%fused_computation.36 | convolution fusion | flops 974860288 | bytes 6848512 | tf_op jit(solution)/shard_map/dot_general | solution.py:68
  118.8 5.9 %all-to-all-done.3 = bf16[2,464,128]{2,1,0:T(8,128)(2,1)S(1)} async-done(((bf16[2,464,128]{2,1,0:T(8,128)(2,1)}), bf16[2,464,128]{2,1,0:T(8,128)(2,1)S(1)}, u32[]{:S(2)}, u32[]{:S(2)}) %all-to-all-start.3) | async-done | bytes 237600 | tf_op jit(solution)/shard_map/all_to_all | solution.py:65
  124.7 0.7 convert_reduce_fusion
  (5 shorter events, 0.1 us)
Async XLA Ops:
  0.6 32.3 %copy-start = (bf16[8,4096]{1,0:T(8,128)(2,1)S(1)}, bf16[8,4096]{1,0:T(8,128)(2,1)}, u32[]{:S(2)}) copy-start(bf16[8,4096]{1,0:T(8,128)(2,1)} %param.4) | copy-start | bytes 196612
  2.3 23.4 %all-to-all-start.1 = ((bf16[8,8,512]{2,1,0:T(8,128)(2,1)}), bf16[8,8,512]{2,1,0:T(8,128)(2,1)S(1)}, u32[]{:S(2)}, u32[]{:S(2)}) async-start(bf16[8,8,512]{2,1,0:T(8,128)(2,1)} %reshape.199), calls=%async_computation.1 | async-start | bytes 131072 | tf_op jit(solution)/shard_map/all_to_all | solution.py:46
  27.0 68.4 %all-to-all-start = ((bf16[8,464,256]{2,1,0:T(8,128)(2,1)}), bf16[8,464,256]{2,1,0:T(8,128)(2,1)}, u32[]{:S(2)}, u32[]{:S(2)}) async-start(bf16[8,464,256]{2,1,0:T(8,128)(2,1)} %broadcast_in_dim.10), calls=%async_computation | async-start | bytes 3801088 | tf_op jit(solution)/shard_map/all_to_all | solution.py:50
  98.7 15.9 %copy-start.1 = (bf16[256,464]{0,1:T(8,128)(2,1)S(1)}, bf16[256,464]{0,1:T(8,128)(2,1)}, u32[]{:S(2)}) copy-start(bf16[256,464]{0,1:T(8,128)(2,1)} %param.6) | copy-start | bytes 712708
  98.7 15.9 %copy-start.2 = (bf16[256,464]{0,1:T(8,128)(2,1)S(1)}, bf16[256,464]{0,1:T(8,128)(2,1)}, u32[]{:S(2)}) copy-start(bf16[256,464]{0,1:T(8,128)(2,1)} %param.5) | copy-start | bytes 712708
  104.9 19.8 %all-to-all-start.3 = ((bf16[2,464,128]{2,1,0:T(8,128)(2,1)}), bf16[2,464,128]{2,1,0:T(8,128)(2,1)S(1)}, u32[]{:S(2)}, u32[]{:S(2)}) async-start(bf16[2,464,128]{2,1,0:T(8,128)(2,1)} %copy.22), calls=%async_computation.3 | async-start | bytes 475136 | tf_op jit(solution)/shard_map/all_to_all | solution.py:65

commit v2 on v1

--- a/solution.py
+++ b/solution.py
@@ -43,15 +43,13 @@
     h, t = hidden.shape
 
     split = grad_out.reshape(8, 2, 8, 256).transpose(2, 0, 1, 3).reshape(8, 8, 512)
-    mine = lax.all_to_all(split, "x", 0, 0)
+    mine = lax.all_to_all(jnp.broadcast_to(split[:, None], (8, 4, 8, 512)).reshape(32, 8, 512), ("x", "zl"), 0, 0)
     own = grad_out.reshape(8, 8, 512).transpose(1, 0, 2)
-    both = jnp.concatenate([own, mine], 0)
-    near = lax.all_gather(both, "zl", axis=1)
+    near = lax.all_gather(own, "zl", axis=1)
     hiddens = lax.all_to_all(jnp.broadcast_to(hidden[None], (8, h, t)), "x", 0, 0)
 
-    near = near.reshape(64, 8, 512)
-    a, ka = coded(near[:32])
-    b, kb = coded(near[32:])
+    a, ka = coded(near.reshape(32, 8, 512))
+    b, kb = coded(mine)
     message = jnp.concatenate([a, b, ka, kb], 0)
     got = lax.all_gather(message, "y", axis=1, tiled=True).astype(jnp.float32)
     whole = (got[:32] * power(got[64], -1)).astype(jnp.bfloat16)

time: 126 us -> 127 us (level)
  waiting for transfers between devices: 11.7 us -> 5.8 us
  blocking collectives: 61.4 us -> 64.8 us
  starting transfers between devices: 32 us -> 35.2 us
    all_to_all x1, waiting for transfers between devices: 5.74 us -> 0.01 us  [body(): lax.all_to_all(jnp.broadcast_to(split[:, None], (8, 4, 8, 512)).reshape(3...]
    all_gather x1, blocking collectives: 42 us -> 45.6 us  [body(): got = lax.all_gather(message, 'y', axis=1, tiled=True).astype(jnp.float32)]
    all_to_all x1, starting transfers between devices: 9.72 us -> 11.2 us  [body(): part = lax.all_to_all(part, 'zh', 0, 0).astype(jnp.float32).sum(0)]
    all_to_all x1, starting transfers between devices: 5.87 us -> 7.28 us  [body(): lax.all_to_all(jnp.broadcast_to(hidden[None], (8, h, t)), 'x', 0, 0)]
  transfers between devices with their start and end apart: 3 -> 3, of which waited for: 2 -> 1; matrix products, arithmetic and copies ran while one was open for 8% -> 8% of each run, Pallas kernels for 0% -> 0%
where the time goes in v2:
time: 127 us; the launch traced here: 126 us
  blocking collectives  64.8 us (51%)
  starting transfers between devices  35.2 us (28%)
  other arithmetic  8 us (6%)
  matrix products  7.41 us (6%)
  waiting for transfers between devices  5.8 us (5%)
  local copies, waits for them, and re-layouts  4.18 us (3%)
    all_gather x1, blocking collectives, body(): got = lax.all_gather(message, 'y', axis=1, tiled=True).astype(jnp.float32)  45.6 us
    all_to_all x1, starting transfers between devices, body(): lax.all_to_all(jnp.broadcast_to(split[:, None], (8, 4, 8, 512)).reshape(3...  16.7 us
    all_gather x1, blocking collectives, body(): near = lax.all_gather(own, 'zl', axis=1)  15.1 us
    all_to_all x1, starting transfers between devices, body(): part = lax.all_to_all(part, 'zh', 0, 0).astype(jnp.float32).sum(0)  11.2 us
    all_to_all x1, starting transfers between devices, body(): lax.all_to_all(jnp.broadcast_to(hidden[None], (8, h, t)), 'x', 0, 0)  7.28 us
    all_to_all x1, waiting for transfers between devices, body(): part = lax.all_to_all(part, 'zh', 0, 0).astype(jnp.float32).sum(0)  5.79 us
    dot_general x1, matrix products, body(): lax.dot_general(weight, whole, (((1, 2), (0, 2)), ((), ())), preferred_el...  4.11 us
    all_to_all x1, blocking collectives, body(): lax.all_to_all(part, 'c', 0, 0).astype(jnp.float32).sum(0)  4.09 us
  transfers between devices with their start and end apart: 3, of which 1 were waited for; matrix products, arithmetic and copies ran while one was open for 8% of the time, Pallas kernels for 0%

profile of v2, /device:TPU:2, one launch (start us, length us, event | category | flops | bytes accessed | tf_op | source)
XLA Modules:
  0.0 126.1 jit_solution(8080674080818619119)
XLA Ops:
  0.6 0.9 copy.37
  1.6 0.7 broadcast_in_dim.34
  2.3 16.7 %all-to-all-start.1 = ((bf16[32,8,512]{2,1,0:T(8,128)(2,1)}), bf16[32,8,512]{2,1,0:T(8,128)(2,1)S(1)}, u32[]{:S(2)}, u32[]{:S(2)}) async-start(bf16[32,8,512]{2,1,0:T(8,128)(2,1)} %bitcast.9), calls=%async_computation.1 | async-start | bytes 524288 | tf_op jit(solution)/shard_map/all_to_all | solution.py:46
  19.0 15.1 %all-gather = bf16[8,32,512]{2,1,0:T(8,128)(2,1)S(1)} all-gather(bf16[8,8,512]{2,1,0:T(8,128)(2,1)} %bitcast.123), channel_id=2, replica_groups=mesh['zh'=2,'x'=8,'c'=2,'zl'=4,'y'=8] {'zl'}, dimensions={1}, use_global_device_ids=true | all-gather | bytes 327680 | tf_op jit(solution)/shard_map/all_gather | solution.py:48
  34.2 0.1 bitcast_reduce_fusion.1
  34.3 0.1 multiply_select_fusion.15
  34.4 0.1 bitcast_convert_fusion.1
  34.5 0.1 multiply_convert_fusion
  34.5 1.2 fusion.14
  35.8 0.0 all-to-all-done.1
  35.8 1.4 %broadcast_in_dim.14 = bf16[8,464,256]{2,1,0:T(8,128)(2,1)} broadcast(bf16[464,256]{1,0:T(8,128)(2,1)S(1)} %fusion.14), dimensions={1,2} | broadcast | bytes 2138112 | tf_op jit(solution)/shard_map/broadcast_in_dim | solution.py:49
  37.2 7.3 %all-to-all-start = ((bf16[8,464,256]{2,1,0:T(8,128)(2,1)}), bf16[8,464,256]{2,1,0:T(8,128)(2,1)}, u32[]{:S(2)}, u32[]{:S(2)}) async-start(bf16[8,464,256]{2,1,0:T(8,128)(2,1)} %broadcast_in_dim.14), calls=%async_computation | async-start | bytes 3801088 | tf_op jit(solution)/shard_map/all_to_all | solution.py:49
  44.5 0.1 bitcast_reduce_fusion
  44.6 0.1 bitcast_convert_fusion
  44.7 0.1 multiply_select_fusion.10
  44.8 0.1 fusion.12
  44.9 0.2 pad_maximum_fusion
  45.1 45.6 %all-gather.2 = f16[66,64,512]{2,1,0:T(8,128)(2,1)S(1)} all-gather(f16[66,8,512]{2,1,0:T(8,128)(2,1)S(1)} %pad_maximum_fusion), channel_id=1, replica_groups=mesh['zh'=2,'x'=8,'c'=2,'zl'=4,'y'=8] {'y'}, dimensions={1}, use_global_device_ids=true | all-gather | bytes 4866048 | tf_op jit(solution)/shard_map/all_gather | solution.py:54
  90.7 1.2 convert_element_type.97
  91.8 0.2 fusion.30
  92.1 2.7 %fusion = (bf16[32,64,512]{2,1,0:T(8,128)(2,1)S(1)}, bf16[32,64,512]{2,1,0:T(8,128)(2,1)}) fusion(f32[66,64,512]{2,1,0:T(8,128)S(1)} %convert_element_type.97, f32[64,512]{1,0:T(8,128)S(1)} %get-tuple-element.5, f32[64,512]{1,0:T(8,128)S(1)} %get-tuple-element.6), kind=kLoop, calls=%fused_computation.1 | loop fusion | flops 4194304 | bytes 12845056 | tf_op jit(solution)/shard_map/convert_element_type | solution.py:55
  94.8 0.0 all-to-all-done
  94.8 3.3 %fusion.5 = bf16[464,512]{1,0:T(8,128)(2,1)S(1)} fusion(bf16[8,464,256]{2,1,0:T(8,128)(2,1)} %all-to-all-done, bf16[8,256,512]{2,1,0:T(8,128)(2,1)} %bitcast.120), kind=kOutput, calls=%fused_computation.8 | convolution fusion | flops 973316096 | bytes 4472832 | tf_op jit(solution)/shard_map/dot_general | solution.py:60
  98.1 0.0 copy-start
  98.1 0.0 copy-start.1
  98.1 0.1 reshape.197
  98.2 0.2 copy.36
  98.5 4.1 %all_to_all.20 = bf16[2,2,464,128]{3,1,2,0:T(2,128)(2,1)S(1)} all-to-all(bf16[2,2,464,128]{3,1,2,0:T(2,128)(2,1)S(1)} %bitcast.121), channel_id=1, replica_groups=mesh['zh'=2,'x'=8,'c'=2,'zl'=4,'y'=8] {'c'}, dimensions={0} | all-to-all | bytes 950272 | tf_op jit(solution)/shard_map/all_to_all | solution.py:62
  102.6 1.0 reduce_sum.21
  103.6 0.7 copy.22
  104.3 11.2 %all-to-all-start.3 = ((bf16[2,464,128]{2,1,0:T(8,128)(2,1)}), bf16[2,464,128]{2,1,0:T(8,128)(2,1)S(1)}, u32[]{:S(2)}, u32[]{:S(2)}) async-start(bf16[2,464,128]{2,1,0:T(8,128)(2,1)} %copy.22), calls=%async_computation.3 | async-start | bytes 475136 | tf_op jit(solution)/shard_map/all_to_all | solution.py:63
  115.5 0.0 copy-done
  115.5 0.0 copy-done.1
  115.5 4.1 %fusion.26 = (bf16[256,464]{0,1:T(8,128)(2,1)}, bf16[256,464]{0,1:T(8,128)(2,1)}) fusion(bf16[256,464]{0,1:T(8,128)(2,1)S(1)} %copy-done.1, bf16[256,464]{0,1:T(8,128)(2,1)S(1)} %copy-done, bf16[8,256,512]{2,1,0:T(8,128)(2,1)S(1)} %bitcast.119, bf16[58,8,8,512]{3,2,1,0:T(8,128)(2,1)} %bitcast.126), kind=kOutput, calls=%fused_computation.38 | convolution fusion | flops 974860288 | bytes 6848512 | tf_op jit(solution)/shard_map/dot_general | solution.py:66
  119.6 5.8 %all-to-all-done.3 = bf16[2,464,128]{2,1,0:T(8,128)(2,1)S(1)} async-done(((bf16[2,464,128]{2,1,0:T(8,128)(2,1)}), bf16[2,464,128]{2,1,0:T(8,128)(2,1)S(1)}, u32[]{:S(2)}, u32[]{:S(2)}) %all-to-all-start.3) | async-done | bytes 237600 | tf_op jit(solution)/shard_map/all_to_all | solution.py:63
  125.4 0.7 convert_reduce_fusion
  (7 shorter events, 0.2 us)
Async XLA Ops:
  2.3 33.4 %all-to-all-start.1 = ((bf16[32,8,512]{2,1,0:T(8,128)(2,1)}), bf16[32,8,512]{2,1,0:T(8,128)(2,1)S(1)}, u32[]{:S(2)}, u32[]{:S(2)}) async-start(bf16[32,8,512]{2,1,0:T(8,128)(2,1)} %bitcast.9), calls=%async_computation.1 | async-start | bytes 524288 | tf_op jit(solution)/shard_map/all_to_all | solution.py:46
  37.2 57.6 %all-to-all-start = ((bf16[8,464,256]{2,1,0:T(8,128)(2,1)}), bf16[8,464,256]{2,1,0:T(8,128)(2,1)}, u32[]{:S(2)}, u32[]{:S(2)}) async-start(bf16[8,464,256]{2,1,0:T(8,128)(2,1)} %broadcast_in_dim.14), calls=%async_computation | async-start | bytes 3801088 | tf_op jit(solution)/shard_map/all_to_all | solution.py:49
  98.1 17.4 %copy-start = (bf16[256,464]{0,1:T(8,128)(2,1)S(1)}, bf16[256,464]{0,1:T(8,128)(2,1)}, u32[]{:S(2)}) copy-start(bf16[256,464]{0,1:T(8,128)(2,1)} %param.6) | copy-start | bytes 712708
  98.1 17.4 %copy-start.1 = (bf16[256,464]{0,1:T(8,128)(2,1)S(1)}, bf16[256,464]{0,1:T(8,128)(2,1)}, u32[]{:S(2)}) copy-start(bf16[256,464]{0,1:T(8,128)(2,1)} %param.5) | copy-start | bytes 712708
  104.3 21.1 %all-to-all-start.3 = ((bf16[2,464,128]{2,1,0:T(8,128)(2,1)}), bf16[2,464,128]{2,1,0:T(8,128)(2,1)S(1)}, u32[]{:S(2)}, u32[]{:S(2)}) async-start(bf16[2,464,128]{2,1,0:T(8,128)(2,1)} %copy.22), calls=%async_computation.3 | async-start | bytes 475136 | tf_op jit(solution)/shard_map/all_to_all | solution.py:63
